TPU v7x, 32 devices: a whole 2x2x4 slice. The times are simulated.
32 devices in a mesh: replica: 2 (over x), batch: 16 (over z, y, core).
Axes of the slice: x: 2, y: 2, z: 4, core: 2. Of those that a mesh axis runs over, the one named last changes fastest.
Arguments:
- cache_state: bfloat16 [256, 12, 64, 128], P(('replica', 'batch')), parts along dimension 0, may hold values from -6 to 6
- prefill_state: bfloat16 [64, 12, 64, 128], P(('replica', 'batch')), parts along dimension 0, may hold values from -6 to 6
- x_in: bfloat16 [256, 768], P(('replica', 'batch')), parts along dimension 0, may hold values from -6 to 6
- z_in: bfloat16 [256, 768], P(('replica', 'batch')), parts along dimension 0, may hold values from -6 to 6
- b_in: bfloat16 [256, 128], P(('replica', 'batch')), parts along dimension 0, may hold values from -6 to 6
- c_in: bfloat16 [256, 128], P(('replica', 'batch')), parts along dimension 0, may hold values from -0.59765625 to 0.59765625
- dt_in: bfloat16 [256, 12], P(('replica', 'batch')), parts along dimension 0, may hold values from -4 to 4
- dt_bias: float32 [12], replicated, may hold values from -3 to 0.5
- a_log: float32 [12], replicated, may hold values from 0 to 2.5
- d_skip: float32 [12], replicated, may hold values from 0.5 to 1.5
- norm_gain: float32 [768], replicated, may hold values from 0.25 to 1.75
- out_weight: bfloat16 [768, 4096], replicated, may hold values from -0.21875 to 0.21875
- active: int32 [256], P(('replica', 'batch')), parts along dimension 0, may hold values from 0 to 1, as said below
- prefill_count: int32 [32], P(('replica', 'batch')), parts along dimension 0, may hold values from 0 to 2, as said below
- dest_owner: int32 [64], P(('replica', 'batch')), parts along dimension 0, may hold values from 0 to 15, as said below
- dest_slot: int32 [64], P(('replica', 'batch')), parts along dimension 0, may hold values from 0 to 7, as said below
Outputs:
- mixed: bfloat16 [256, 4096], P(('replica', 'batch')), parts along dimension 0
- new_state: bfloat16 [256, 12, 64, 128], P(('replica', 'batch')), parts along dimension 0
There are 2 independent parts, one for each index of `replica`. A program takes and returns all parts, laid end to end along the dimension named above; an argument that names none is the same for every part. Nothing has to cross between parts.
Inputs may be any that keep to these rules, and one draw needn't show every extreme that they name: `active`: at least 2 slots of every device are 0. `prefill_count`: the live rows of a device are its first ones. `dest_owner`: for each row index j below 2, the rows j of the devices go to distinct owners; the two rows of one device go to different owners. So an owner receives at most 2 live rows, at most one from any device, and some owner exactly 2. `dest_slot`: A live row's slot is 0 in the owner's active entries, and no two live rows share an owner and slot.
All inputs are finite; a program needn't handle non-finite values.
Results may differ from a plain program's by a relative error of at most 0.0049.
Values may be sent and summed in bfloat16 or wider, within the bound.
A program may use at most 128 MiB of HBM per device.

v0:
```python
import jax
import jax.numpy as jnp
from jax import lax
from jax.sharding import PartitionSpec as P


def advance(
    state, x_in, z_in, b_in, c_in, dt_in, dt_bias, a_log, d_skip, norm_gain, out_weight, live
):
    rows, heads, hdim, nstate = state.shape
    step = jax.nn.softplus(dt_in.astype(jnp.float32) + dt_bias[None, :])
    decay = jnp.exp(-step * jnp.exp(a_log)[None, :])
    inputs = x_in.astype(jnp.float32).reshape(rows, heads, hdim)
    b_vals = b_in.astype(jnp.float32)
    c_vals = c_in.astype(jnp.float32)
    fresh = (
        state * decay[:, :, None, None]
        + (step[:, :, None] * inputs)[:, :, :, None] * b_vals[:, None, None, :]
    )
    ys = (
        jnp.einsum("rhpn,rn->rhp", fresh, c_vals, precision=lax.Precision.HIGHEST)
        + d_skip[None, :, None] * inputs
    )
    gated = ys.reshape(rows, heads * hdim) * jax.nn.silu(z_in.astype(jnp.float32))
    scale = lax.rsqrt(jnp.mean(gated * gated, axis=1, keepdims=True) + 1e-05)
    normed = jnp.where(live[:, None], gated * scale * norm_gain[None, :], 0.0).astype(jnp.bfloat16)
    mixed = jnp.dot(normed, out_weight, preferred_element_type=jnp.float32).astype(jnp.bfloat16)
    new_state = jnp.where(live[:, None, None, None], fresh, 0.0).astype(jnp.bfloat16)
    return (mixed, new_state)


def body(
    cache_state,
    prefill_state,
    x_in,
    z_in,
    b_in,
    c_in,
    dt_in,
    dt_bias,
    a_log,
    d_skip,
    norm_gain,
    out_weight,
    active,
    prefill_count,
    dest_owner,
    dest_slot,
):
    myself = lax.axis_index("batch")
    slots, heads, hdim, nstate = cache_state.shape
    fresh_rows = prefill_state.shape[0]
    valid = jnp.arange(fresh_rows, dtype=jnp.int32) < prefill_count[0]
    owner_local = jnp.where(valid, dest_owner, -1)
    owner_all, slot_all = (
        lax.all_gather(owner_local, "batch", axis=0, tiled=True),
        lax.all_gather(dest_slot, "batch", axis=0, tiled=True),
    )
    slot_ids = jnp.arange(slots, dtype=jnp.int32)
    onehot = ((owner_all[None, :] == myself) & (slot_all[None, :] == slot_ids[:, None])).astype(
        jnp.bfloat16
    )
    moved = jnp.einsum(
        "sr,rhpn->shpn",
        onehot,
        lax.all_gather(prefill_state, "batch", axis=0, tiled=True),
        preferred_element_type=jnp.float32,
    )
    arrived = jnp.sum(onehot.astype(jnp.float32), axis=1)
    landed = arrived > 0.5
    live = (active > 0) | landed
    state = jnp.where(landed[:, None, None, None], moved, cache_state.astype(jnp.float32))
    return advance(
        state, x_in, z_in, b_in, c_in, dt_in, dt_bias, a_log, d_skip, norm_gain, out_weight, live
    )


def solution(mesh):
    in_specs = (
        P(("replica", "batch"), None, None, None),
        P(("replica", "batch"), None, None, None),
        P(("replica", "batch"), None),
        P(("replica", "batch"), None),
        P(("replica", "batch"), None),
        P(("replica", "batch"), None),
        P(("replica", "batch"), None),
        P(),
        P(),
        P(),
        P(),
        P(),
        P(("replica", "batch")),
        P(("replica", "batch")),
        P(("replica", "batch")),
        P(("replica", "batch")),
    )
    out_specs = (P(("replica", "batch"), None), P(("replica", "batch"), None, None, None))
    return jax.shard_map(body, mesh=mesh, in_specs=in_specs, out_specs=out_specs, check_vma=False)
```

profile of v0, /device:TPU:1, one launch (start us, length us, event | category | flops | bytes accessed | tf_op | source)
XLA Modules:
  0.0 99.7 jit_solution(15233405479906847518)
XLA Ops:
  7.2 0.0 copy-start
  7.2 0.0 all-gather.2.cloned.1.call-start
  7.2 0.7 all-gather.2.cloned.1.call-update
  8.6 0.7 exp.15
  9.2 0.7 convert_element_type.33
  9.9 0.7 multiply_exponential_fusion
  10.6 0.1 copy.31
  10.7 0.8 reshape.45
  11.5 0.1 broadcast_multiply_fusion
  11.6 0.2 copy.32
  11.8 1.2 %dynamic-slice = u32[1]{0:T(128)} dynamic-slice(u32[32]{0:T(128)} %constant.35, u32[]{:T(128)S(6)} %add.37), dynamic_slice_sizes={1} | dynamic-slice | bytes 12
  13.7 0.9 dynamic-update-slice.1
  14.6 0.7 fusion.21
  15.3 11.8 %all-reduce.2 = (s32[32]{0:T(128)S(1)}, s32[32]{0:T(128)S(1)}) all-reduce(s32[32]{0:T(128)S(1)} %dynamic-update-slice.1, s32[32]{0:T(128)S(1)} %fusion.21), channel_id=1, replica_groups=mesh['replica'=2,'batch'=16] {'batch'}, use_global_device_ids=true, to_apply=%add.1 | all-reduce | flops 64 | bytes 512
  27.1 0.1 convert_reduce_fusion
  27.2 0.7 compare_or_fusion
  27.9 46.4 %all-gather.2.cloned.1.call-done = bf16[32,12,64,128]{3,2,1,0:T(8,128)(2,1)} async-done(((bf16[2,12,64,128]{3,2,1,0:T(8,128)(2,1)}), bf16[32,12,64,128]{3,2,1,0:T(8,128)(2,1)}) %all-gather.2.cloned.1.call-update) | async-done | bytes 6291472 | tf_op jit(solution)/shard_map/all_gather | solution.py:66
  74.3 8.4 %select_convert_fusion = (bf16[8,12,64,128]{3,0,2,1:T(8,128)(2,1)S(1)}, f32[8,12,64,128]{3,0,2,1:T(8,128)S(1)}) fusion(pred[8]{0:T(512)(128)(4,1)S(1)} %get-tuple-element.12, f32[8,128]{1,0:T(8,128)S(1)} %convert_element_type.33, f32[8,12,64]{0,2,1:T(8,128)S(1)} %copy.32, f32[8,12]{0,1:T(8,128)S(1)} %copy.31, bf16[8,12,64,128]{3,2,1,0:T(8,128)(2,1)} %param.16, ...), kind=kOutput, calls=%fused_computation.5 | convolution fusion | flops 55050752 | bytes 12612144 | tf_op jit(solution)/shard_map/sr,rhpn->shpn/dot_general | solution.py:63
  82.7 0.0 copy-start.3
  82.8 0.0 copy-start.1
  82.8 0.0 copy-start.2
  82.8 1.6 %copy.33 = bf16[8,12,64,128]{3,2,1,0:T(8,128)(2,1)} copy(bf16[8,12,64,128]{3,0,2,1:T(8,128)(2,1)S(1)} %get-tuple-element.14) | data formatting | bytes 3145728
  84.3 0.0 copy-done
  84.3 3.8 %fusion.2 = f32[8,1,12,64]{3,1,2,0:T(1,128)S(1)} fusion(f32[8,12,64,128]{3,0,2,1:T(8,128)S(1)} %get-tuple-element.15, bf16[8,128,1,1]{1,0,2,3:T(8,128)(2,1)S(1)} %bitcast.14), kind=kOutput, calls=%fused_computation.3 | convolution fusion | flops 9437184 | bytes 3172352 | tf_op jit(solution)/shard_map/rhpn,rn->rhp/dot_general | solution.py:21
  88.1 0.0 copy-done.3
  88.1 0.1 bitcast_add_fusion
  88.2 0.1 reshape.43
  88.3 0.0 copy-done.1
  88.3 0.1 multiply_reduce_fusion
  88.4 0.0 copy-done.2
  88.4 4.4 %convolution_convert_fusion = bf16[8,4096]{1,0:T(8,128)(2,1)} fusion(bf16[768,4096]{1,0:T(8,128)(2,1)} %param.27, f32[768]{0:T(1024)S(1)} %copy-done.2, f32[8]{0:T(128)S(1)} %add_rsqrt_fusion, pred[8]{0:T(512)(128)(4,1)S(1)} %get-tuple-element.12, f32[8,768]{1,0:T(8,128)S(1)} %reshape.43, bf16[8,768]{1,0:T(8,128)(2,1)S(1)} %copy-done.1), kind=kOutput, calls=%fused_computation.2 | convolution fusion | flops 50425856 | bytes 6396968 | tf_op jit(solution)/shard_map/dot_general | solution.py:27
  (4 shorter events, 0.0 us)
Async XLA Ops:
  7.2 77.2 %copy-start = (bf16[8,128]{1,0:T(8,128)(2,1)S(1)}, bf16[8,128]{1,0:T(8,128)(2,1)}, u32[]{:S(2)}) copy-start(bf16[8,128]{1,0:T(8,128)(2,1)} %param.21) | copy-start | bytes 6148
  7.2 67.1 %all-gather.2.cloned.1.call-start = ((), (), s32[]{:S(2)}) async-start(), calls=%async_computation | async-start | bytes 6684672 | tf_op jit(solution)/shard_map/all_gather | solution.py:66
  82.7 5.4 %copy-start.3 = (f32[12]{0:T(128)S(1)}, f32[12]{0:T(128)}, u32[]{:S(2)}) copy-start(f32[12]{0:T(128)} %param.25) | copy-start | bytes 148
  82.8 5.5 %copy-start.1 = (bf16[8,768]{1,0:T(8,128)(2,1)S(1)}, bf16[8,768]{1,0:T(8,128)(2,1)}, u32[]{:S(2)}) copy-start(bf16[8,768]{1,0:T(8,128)(2,1)} %param.19) | copy-start | bytes 36868
  82.8 5.7 %copy-start.2 = (f32[768]{0:T(1024)S(1)}, f32[768]{0:T(1024)}, u32[]{:S(2)}) copy-start(f32[768]{0:T(1024)} %param.26) | copy-start | bytes 9220
Sparse Core Ops, SparseCore 0:
  10.3 63.9 all-gather.1
where the time goes:
time: 100 us; the launch traced here: 99.7 us
  waiting for transfers between devices  47.1 us (47%)
  matrix products  16.6 us (17%)
  between operations  15.4 us (15%)
  blocking collectives  11.8 us (12%)
  local copies, waits for them, and re-layouts  5.49 us (5%)
  other arithmetic  3.25 us (3%)
    all_gather x1, waiting for transfers between devices, body(): lax.all_gather(prefill_state, 'batch', axis=0, tiled=True)  46.4 us
    unnamed x1, blocking collectives  11.8 us
    dot_general x1, matrix products, body(): jnp.einsum('sr,rhpn->shpn', onehot, lax.all_gather(prefill_state, 'batch'...  8.45 us
    dot_general x1, matrix products, advance(): jnp.dot(normed, out_weight, preferred_element_type=jnp.float32)  4.39 us
    dot_general x1, matrix products, advance(): jnp.einsum('rhpn,rn->rhp', fresh, c_vals, precision=lax.Precision.HIGHEST)  3.76 us
    unnamed x13, local copies, waits for them, and re-layouts  3.69 us
  transfers between devices with their start and end apart: 1, of which 1 were waited for; matrix products, arithmetic and copies ran while one was open for 7% of the time, Pallas kernels for 0%

commit v1 on v0

v1 whole, which is shorter than its diff:
```python
import functools

import jax
import jax.numpy as jnp
from jax import lax
from jax.experimental import pallas as pl
from jax.experimental.pallas import tpu as pltpu
from jax.sharding import PartitionSpec as P

MESH = pl.DeviceIdType.MESH
ROOM = 24 * 1024 * 1024


def gather_kernel(
    n, meta_ref, pre_ref, moved_ref, info_ref, buf, meta_buf, meta_smem,
    recv_sem, left_sem, right_sem, across_sem, mate_sem, local_sem,
):
    depth = n // 4
    rows = pre_ref.shape[0]
    me = lax.axis_index("batch")
    z, y, c = me // 4, (me // 2) % 2, me % 2

    def index(zz, yy, cc):
        return (zz * 2 + yy) * 2 + cc

    left, right = index(z - 1, y, c), index(z + 1, y, c)
    across, mate = index(z, 1 - y, c), index(z, y, 1 - c)
    has_left, has_right = z > 0, z < depth - 1

    barrier = pltpu.get_barrier_semaphore()

    def greet(other):
        pl.semaphore_signal(barrier, inc=1, device_id={"batch": other}, device_id_type=MESH)

    greet(across)
    greet(mate)
    pl.when(has_left)(lambda: greet(left))
    pl.when(has_right)(lambda: greet(right))
    pl.semaphore_wait(barrier, 2 + has_left.astype(jnp.int32) + has_right.astype(jnp.int32))

    def slot(o, j):
        return meta_buf.at[o] if j == rows else buf.at[o, j]

    def mine(j):
        return meta_ref if j == rows else pre_ref.at[j]

    sent = []

    def send(cond, src, o, j, sem, target):
        copy = pltpu.make_async_remote_copy(
            src_ref=src, dst_ref=slot(o, j), send_sem=sem, recv_sem=recv_sem.at[o, j],
            device_id={"batch": target}, device_id_type=MESH,
        )
        if cond is None:
            copy.start()
        else:
            pl.when(cond)(copy.start)
        sent.append((cond, copy))

    def arrive(o, j):
        pltpu.make_async_remote_copy(
            src_ref=slot(o, j), dst_ref=slot(o, j), send_sem=local_sem.at[0],
            recv_sem=recv_sem.at[o, j], device_id={"batch": mate}, device_id_type=MESH,
        ).wait_recv()

    def both(*conds):
        return functools.reduce(jnp.logical_and, conds)

    order = (rows,) + tuple(range(rows))
    last = rows - 1
    for j in order:
        send(has_left, mine(j), me, j, left_sem.at[z, j], left)
        send(has_right, mine(j), me, j, right_sem.at[z, j], right)
    for j in (rows,) + tuple(reversed(range(rows))):
        send(None, mine(j), me, j, across_sem.at[z, j], across)
    for j in order:
        send(None, mine(j), me, j, mate_sem.at[z * 2 + y, j], mate)
    own_rows = pltpu.make_async_copy(pre_ref, buf.at[me], local_sem.at[1])
    own_meta = pltpu.make_async_copy(meta_ref, meta_buf.at[me], local_sem.at[2])
    own_rows.start()
    own_meta.start()

    def from_across(t):
        for sign in (1, -1) if t else (1,):
            zz = z + t * sign
            o = index(zz, 1 - y, c)
            inside = both(zz >= 0, zz < depth) if t else None
            for j in (rows,) + tuple(reversed(range(rows))):
                cond = inside
                if t and j == last:
                    cond = both(inside, zz > 0, zz < depth - 1)
                if cond is None:
                    arrive(o, j)
                else:
                    pl.when(cond)(functools.partial(arrive, o, j))
                if not t and j == last:
                    send(both(z == depth - 1, has_left), slot(o, j), o, j, left_sem.at[depth, j], left)
                    send(both(z == 0, has_right), slot(o, j), o, j, right_sem.at[depth, j], right)
                send(cond, slot(o, j), o, j, mate_sem.at[zz * 2 + 1 - y, j], mate)

    for s in range(1, depth):
        for j in order:
            for sign in (1, -1):
                zz = z + s * sign
                o = index(zz, y, c)
                inside = both(zz >= 0, zz < depth)
                pl.when(inside)(functools.partial(arrive, o, j))
                if sign == 1:
                    send(both(inside, has_left), slot(o, j), o, j, left_sem.at[zz, j], left)
                else:
                    send(both(inside, has_right), slot(o, j), o, j, right_sem.at[zz, j], right)
                cond = both(inside, zz > 0, zz < depth - 1) if j == last else inside
                send(cond, slot(o, j), o, j, across_sem.at[zz, j], across)
                send(inside, slot(o, j), o, j, mate_sem.at[zz * 2 + y, j], mate)
        from_across(s - 1)
    if depth > 1:
        o = index(depth - 1, 1 - y, c)
        pl.when(has_right)(functools.partial(arrive, o, last))
        send(both(has_right, has_left), slot(o, last), o, last, left_sem.at[depth, last], left)
        send(has_right, slot(o, last), o, last, mate_sem.at[(depth - 1) * 2 + 1 - y, last], mate)
        o = index(0, 1 - y, c)
        pl.when(has_left)(functools.partial(arrive, o, last))
        send(both(has_right, has_left), slot(o, last), o, last, right_sem.at[depth, last], right)
        send(has_left, slot(o, last), o, last, mate_sem.at[1 - y, last], mate)
    from_across(depth - 1)
    own_rows.wait()
    own_meta.wait()

    def of_mate(j):
        def one(k, carry):
            arrive(k * 2 + 1 - c, j)
            return carry
        lax.fori_loop(0, 2 * depth, one, 0)

    of_mate(rows)
    numbers = pltpu.make_async_copy(meta_buf, meta_smem, local_sem.at[3])
    numbers.start()
    numbers.wait()

    picks = []
    for j in range(rows):
        def look(d, carry, j=j):
            hit = meta_smem[d, 0, j] == me
            source, place = carry
            return jnp.where(hit, d, source), jnp.where(hit, meta_smem[d, 0, rows + j], place)
        source, place = lax.fori_loop(0, n, look, (jnp.int32(0), jnp.int32(-1)))
        picks.append(source)
        info_ref[j] = place
    for j in range(rows):
        of_mate(j)
    for j in range(rows):
        moved_ref[j] = buf[picks[j], j]
    for cond, copy in sent:
        if cond is None:
            copy.wait_send()
        else:
            pl.when(cond)(copy.wait_send)


def gather_rows(meta, prefill_state, n):
    rows = prefill_state.shape[0]
    depth = n // 4
    dma = pltpu.SemaphoreType.DMA
    vmem = pl.BlockSpec(memory_space=pltpu.VMEM)
    return pl.pallas_call(
        functools.partial(gather_kernel, n),
        out_shape=(
            jax.ShapeDtypeStruct(prefill_state.shape, prefill_state.dtype),
            jax.ShapeDtypeStruct((rows,), jnp.int32),
        ),
        in_specs=[vmem, vmem],
        out_specs=(vmem, pl.BlockSpec(memory_space=pltpu.SMEM)),
        scratch_shapes=[
            pltpu.VMEM((n,) + prefill_state.shape, prefill_state.dtype),
            pltpu.VMEM((n,) + meta.shape, jnp.int32),
            pltpu.SMEM((n,) + meta.shape, jnp.int32),
            dma((n, rows + 1)),
            dma((depth + 1, rows + 1)),
            dma((depth + 1, rows + 1)),
            dma((depth, rows + 1)),
            dma((2 * depth, rows + 1)),
            dma((4,)),
        ],
        compiler_params=pltpu.CompilerParams(
            collective_id=0, has_side_effects=True, vmem_limit_bytes=ROOM + 4 * 1024 * 1024
        ),
        name="gather_rows",
    )(meta, prefill_state)


def step_kernel(
    info_ref, active_ref, cache_ref, moved_ref, weight_ref, x_ref, z_ref, b_ref, c_ref, dt_ref,
    bias_ref, log_ref, skip_ref, gain_ref, mixed_ref, new_ref, states, fresh, weight,
    step_rows, decay_rows, in_sem, out_sem, weight_sem,
):
    slots, heads, hdim, nstate = cache_ref.shape
    inner = heads * hdim
    moves = moved_ref.shape[0]
    f32 = jnp.float32

    def load(r):
        hit = [info_ref[j] == r for j in range(moves)]
        held = functools.reduce(jnp.logical_or, hit)
        for j in range(moves):
            pl.when(hit[j])(
                pltpu.make_async_copy(moved_ref.at[j], states.at[r], in_sem.at[r]).start
            )
        pl.when(jnp.logical_not(held))(
            pltpu.make_async_copy(cache_ref.at[r], states.at[r], in_sem.at[r]).start
        )
        return jnp.where(jnp.logical_or(held, active_ref[r] > 0), 1.0, 0.0).astype(f32)

    live_scalars = [load(r) for r in range(slots)]
    weights = pltpu.make_async_copy(weight_ref, weight, weight_sem)
    weights.start()

    row_id = lax.broadcasted_iota(jnp.int32, (slots, 128), 0)
    live = jnp.zeros((slots, 128), f32)
    for r in range(slots):
        live = jnp.where(row_id == r, live_scalars[r], live)

    step = jax.nn.softplus(dt_ref[...].astype(f32) + bias_ref[...])
    decay = jnp.exp(-step * jnp.exp(log_ref[...]))
    step_rows[...] = step * live[:, :heads]
    decay_rows[...] = decay * live[:, :heads]
    spread = jnp.where(
        lax.broadcasted_iota(jnp.int32, (heads, inner), 1) // hdim
        == lax.broadcasted_iota(jnp.int32, (heads, inner), 0), 1.0, 0.0
    ).astype(f32)

    def widen(v):
        return jnp.dot(v, spread, precision=lax.Precision.HIGHEST, preferred_element_type=f32)

    x = x_ref[...]
    b = b_ref[...]
    c = c_ref[...]

    def slot(r, total):
        pltpu.make_async_copy(cache_ref.at[r], states.at[r], in_sem.at[r]).wait()
        here = row_id[:, :nstate] == r
        b_row = jnp.where(here, b.astype(f32), 0.0).astype(jnp.bfloat16)
        c_row = jnp.where(here, c.astype(f32), 0.0).astype(jnp.bfloat16)
        state = states[r]
        flat = state.reshape(inner, nstate)
        total = total + lax.dot_general(
            c_row, flat, (((1,), (1,)), ((), ())), preferred_element_type=f32
        )
        outer = lax.dot_general(x, b_row, (((0,), (0,)), ((), ())), preferred_element_type=f32)
        step_row = step_rows[pl.ds(r, 1), :]
        decay_row = decay_rows[pl.ds(r, 1), :]
        for h in range(heads):
            fresh[r, h] = (
                state[h].astype(f32) * decay_row[:, h : h + 1]
                + outer[h * hdim : (h + 1) * hdim] * step_row[:, h : h + 1]
            ).astype(fresh.dtype)
        pltpu.make_async_copy(fresh.at[r], new_ref.at[r], out_sem.at[r]).start()
        return total

    held = lax.fori_loop(0, slots, slot, jnp.zeros((slots, inner), f32))
    inputs = x.astype(f32)
    mix = jnp.sum(b.astype(f32) * c.astype(f32), axis=1, keepdims=True)
    ys = widen(decay) * held + widen(step) * inputs * mix + widen(skip_ref[...]) * inputs
    gated = ys * jax.nn.silu(z_ref[...].astype(f32))
    scale = lax.rsqrt(jnp.mean(gated * gated, axis=1, keepdims=True) + 1e-05)
    normed = jnp.where(live[:, :1] > 0.5, gated * scale * gain_ref[...], 0.0).astype(jnp.bfloat16)
    weights.wait()
    width = mixed_ref.shape[1]
    tile = 512
    while width % tile:
        tile //= 2

    def columns(k, carry):
        part = pl.ds(pl.multiple_of(k * tile, tile), tile)
        mixed_ref[:, part] = jnp.dot(
            normed, weight[:, part], preferred_element_type=f32
        ).astype(mixed_ref.dtype)
        return carry

    lax.fori_loop(0, width // tile, columns, 0)

    def flush(r, carry):
        pltpu.make_async_copy(fresh.at[r], new_ref.at[r], out_sem.at[r]).wait()
        return carry

    lax.fori_loop(0, slots, flush, 0)


def advance(
    info, active, cache_state, moved, out_weight, x_in, z_in, b_in, c_in, dt_in, dt_bias, a_log,
    d_skip, norm_gain,
):
    slots, heads, hdim, nstate = cache_state.shape
    vmem = pl.BlockSpec(memory_space=pltpu.VMEM)
    smem = pl.BlockSpec(memory_space=pltpu.SMEM)
    hbm = pl.BlockSpec(memory_space=pl.ANY)
    dma = pltpu.SemaphoreType.DMA
    return pl.pallas_call(
        step_kernel,
        out_shape=(
            jax.ShapeDtypeStruct((slots, out_weight.shape[1]), jnp.bfloat16),
            jax.ShapeDtypeStruct(cache_state.shape, jnp.bfloat16),
        ),
        in_specs=[smem, smem, hbm, hbm, hbm] + [vmem] * 9,
        out_specs=(vmem, hbm),
        scratch_shapes=[
            pltpu.VMEM(cache_state.shape, cache_state.dtype),
            pltpu.VMEM(cache_state.shape, jnp.bfloat16),
            pltpu.VMEM(out_weight.shape, out_weight.dtype),
            pltpu.VMEM((slots, heads), jnp.float32),
            pltpu.VMEM((slots, heads), jnp.float32),
            dma((slots,)),
            dma((slots,)),
            dma,
        ],
        compiler_params=pltpu.CompilerParams(vmem_limit_bytes=32 * 1024 * 1024),
        name="decode_step",
    )(
        info, active, cache_state, moved, out_weight, x_in, z_in, b_in, c_in, dt_in,
        dt_bias[None, :], a_log[None, :], d_skip[None, :], norm_gain[None, :],
    )


def body(
    n, cache_state, prefill_state, x_in, z_in, b_in, c_in, dt_in, dt_bias, a_log, d_skip,
    norm_gain, out_weight, active, prefill_count, dest_owner, dest_slot,
):
    rows = prefill_state.shape[0]
    valid = jnp.arange(rows, dtype=jnp.int32) < prefill_count[0]
    owner = jnp.where(valid, dest_owner, -1)
    if n % 4 == 0 and n * prefill_state.size * 2 <= ROOM:
        meta = jnp.concatenate([owner, dest_slot, jnp.zeros((128 - 2 * rows,), jnp.int32)])[None, :]
        moved, info = gather_rows(meta, prefill_state, n)
    else:
        myself = lax.axis_index("batch")
        owners = lax.all_gather(owner, "batch", axis=0)
        places = lax.all_gather(dest_slot, "batch", axis=0)
        states = lax.all_gather(prefill_state, "batch", axis=0)
        hit = owners == myself
        source = jnp.argmax(hit, axis=0)
        column = jnp.arange(rows)
        info = jnp.where(jnp.any(hit, axis=0), places[source, column], -1)
        moved = states[source, column]
    return advance(
        info, active, cache_state, moved, out_weight, x_in, z_in, b_in, c_in, dt_in, dt_bias,
        a_log, d_skip, norm_gain,
    )


def solution(mesh):
    split = ("replica", "batch")
    state, matrix, vector = P(split, None, None, None), P(split, None), P(split)
    in_specs = (state, state) + (matrix,) * 5 + (P(),) * 5 + (vector,) * 4
    return jax.shard_map(
        functools.partial(body, mesh.shape["batch"]), mesh=mesh, in_specs=in_specs,
        out_specs=(matrix, state), check_vma=False,
    )
```

time: 100 us -> 70.8 us (0.71)
  the two profiles are of different devices: /device:TPU:1 before, /device:TPU:27 now
where the time goes in v1:
time: 70.8 us; the launch traced here: 70.4 us
  Pallas kernels  55.7 us (79%)
  local copies, waits for them, and re-layouts  11.9 us (17%)
  other arithmetic  1.39 us (2%)
  between operations  1.31 us (2%)
    pallas_call x1, Pallas kernels, gather_rows(): pl.pallas_call(functools.partial(gather_kernel, n), out_shape=(jax.ShapeD...  47.3 us
    unnamed x24, local copies, waits for them, and re-layouts  11.3 us
    pallas_call x1, Pallas kernels, advance(): pl.pallas_call(step_kernel, out_shape=(jax.ShapeDtypeStruct((slots, out_w...  8.44 us

profile of v1, /device:TPU:27, one launch (start us, length us, event | category | flops | bytes accessed | tf_op | source)
XLA Modules:
  0.0 70.4 jit_solution(16997129152481071850)
XLA Ops:
  1.3 0.7 compare_select_fusion
  1.9 0.7 %add_bitcast_fusion.meta_ref = s32[1,128]{1,0:T(1,128)S(1)} fusion(s32[124]{0:T(128)S(1)} %broadcast_in_dim.23, s32[2]{0:T(128)} %param.31, s32[2]{0:T(128)S(1)} %compare_select_fusion), kind=kLoop, calls=%fused_computation.1 | loop fusion | flops 256 | bytes 1024 | tf_op jit(solution)/shard_map/broadcast_in_dim | solution.py:331
  2.7 0.7 broadcast_in_dim.28.gain_ref
  3.4 0.0 copy-start.2
  3.4 1.0 %copy-done.2 = bf16[2,12,64,128]{3,2,1,0:T(8,128)(2,1)S(1)} copy-done((bf16[2,12,64,128]{3,2,1,0:T(8,128)(2,1)S(1)}, bf16[2,12,64,128]{3,2,1,0:T(8,128)(2,1)}, u32[]{:S(2)}) %copy-start.2) | copy-done | bytes 393240
  4.4 47.3 %gather_rows.1 = (bf16[2,12,64,128]{3,2,1,0:T(8,128)(2,1)S(1)}, s32[2]{0:T(128)S(1)}) custom-call(s32[1,128]{1,0:T(1,128)S(1)} %add_bitcast_fusion.meta_ref, bf16[2,12,64,128]{3,2,1,0:T(8,128)(2,1)S(1)} %copy-done.2), custom_call_target="tpu_custom_call" | custom-call | tf_op jit(solution)/shard_map/gather_rows/pallas_call | solution.py:165
  51.6 0.0 copy-start
  51.6 2.8 %copy-done = bf16[768,4096]{1,0:T(8,128)(2,1)S(1)} copy-done((bf16[768,4096]{1,0:T(8,128)(2,1)S(1)}, bf16[768,4096]{1,0:T(8,128)(2,1)}, u32[]{:S(2)}) %copy-start) | copy-done | bytes 6291480
  54.4 0.0 copy-start.1
  54.4 1.4 %copy-done.1 = bf16[8,12,64,128]{3,2,1,0:T(8,128)(2,1)S(1)} copy-done((bf16[8,12,64,128]{3,2,1,0:T(8,128)(2,1)S(1)}, bf16[8,12,64,128]{3,2,1,0:T(8,128)(2,1)}, u32[]{:S(2)}) %copy-start.1) | copy-done | bytes 1572888
  55.8 0.0 copy-start.3
  55.8 0.7 %copy-done.3 = bf16[8,768]{1,0:T(8,128)(2,1)S(1)} copy-done((bf16[8,768]{1,0:T(8,128)(2,1)S(1)}, bf16[8,768]{1,0:T(8,128)(2,1)}, u32[]{:S(2)}) %copy-start.3) | copy-done | bytes 12312
  56.5 0.0 copy-start.4
  56.5 0.7 %copy-done.4 = bf16[8,768]{1,0:T(8,128)(2,1)S(1)} copy-done((bf16[8,768]{1,0:T(8,128)(2,1)S(1)}, bf16[8,768]{1,0:T(8,128)(2,1)}, u32[]{:S(2)}) %copy-start.4) | copy-done | bytes 12312
  57.2 0.0 copy-start.5
  57.2 0.7 copy-done.5
  57.9 0.0 copy-start.6
  57.9 0.7 copy-done.6
  58.6 0.0 copy-start.7
  58.6 0.7 copy-done.7
  59.3 0.0 copy-start.8
  59.3 0.7 copy-done.8
  59.9 0.0 copy-start.9
  60.0 0.7 copy-done.9
  60.6 0.0 copy-start.10
  60.6 0.7 copy-done.10
  61.3 0.0 copy-start.11
  61.3 0.7 copy-done.11
  61.9 8.4 %decode_step.1 = (bf16[8,4096]{1,0:T(8,128)(2,1)}, bf16[8,12,64,128]{3,2,1,0:T(8,128)(2,1)}) custom-call(s32[2]{0:T(128)S(1)} %get-tuple-element.4.info_ref, s32[8]{0:T(128)S(1)} %copy-done.8, bf16[8,12,64,128]{3,2,1,0:T(8,128)(2,1)S(1)} %copy-done.1, bf16[2,12,64,128]{3,2,1,0:T(8,128)(2,1)S(1)} %get-tuple-element.5.moved_ref, ...), custom_call_target="tpu_custom_call" | custom-call | tf_op jit(solution)/shard_map/decode_step/pallas_call | solution.py:297
  (1 shorter events, 0.0 us)
Async XLA Ops:
  3.4 1.0 %copy-start.2 = (bf16[2,12,64,128]{3,2,1,0:T(8,128)(2,1)S(1)}, bf16[2,12,64,128]{3,2,1,0:T(8,128)(2,1)}, u32[]{:S(2)}) copy-start(bf16[2,12,64,128]{3,2,1,0:T(8,128)(2,1)} %pre_ref.1) | copy-start | bytes 1179652
  51.6 2.8 %copy-start = (bf16[768,4096]{1,0:T(8,128)(2,1)S(1)}, bf16[768,4096]{1,0:T(8,128)(2,1)}, u32[]{:S(2)}) copy-start(bf16[768,4096]{1,0:T(8,128)(2,1)} %weight_ref.1) | copy-start | bytes 18874372
  54.4 1.4 %copy-start.1 = (bf16[8,12,64,128]{3,2,1,0:T(8,128)(2,1)S(1)}, bf16[8,12,64,128]{3,2,1,0:T(8,128)(2,1)}, u32[]{:S(2)}) copy-start(bf16[8,12,64,128]{3,2,1,0:T(8,128)(2,1)} %cache_ref.1) | copy-start | bytes 4718596
  55.8 0.7 %copy-start.3 = (bf16[8,768]{1,0:T(8,128)(2,1)S(1)}, bf16[8,768]{1,0:T(8,128)(2,1)}, u32[]{:S(2)}) copy-start(bf16[8,768]{1,0:T(8,128)(2,1)} %x_ref.1) | copy-start | bytes 36868
  56.5 0.7 %copy-start.4 = (bf16[8,768]{1,0:T(8,128)(2,1)S(1)}, bf16[8,768]{1,0:T(8,128)(2,1)}, u32[]{:S(2)}) copy-start(bf16[8,768]{1,0:T(8,128)(2,1)} %z_ref.1) | copy-start | bytes 36868
  57.2 0.7 copy-start.5
  57.9 0.7 copy-start.6
  58.6 0.7 copy-start.7
  59.3 0.7 copy-start.8
  59.9 0.7 copy-start.9
  60.6 0.7 copy-start.10
  61.3 0.7 copy-start.11

commit v2 on v1

--- a/solution.py
+++ b/solution.py
@@ -8,6 +8,7 @@
 from jax.sharding import PartitionSpec as P
 
 MESH = pl.DeviceIdType.MESH
+VMEM_ALL = 67043328
 ROOM = 24 * 1024 * 1024
 
 
@@ -27,6 +28,8 @@
     across, mate = index(z, 1 - y, c), index(z, y, 1 - c)
     has_left, has_right = z > 0, z < depth - 1
 
+    own_rows = pltpu.make_async_copy(pre_ref, buf.at[me], local_sem.at[1])
+    own_rows.start()
     barrier = pltpu.get_barrier_semaphore()
 
     def greet(other):
@@ -42,7 +45,9 @@
         return meta_buf.at[o] if j == rows else buf.at[o, j]
 
     def mine(j):
-        return meta_ref if j == rows else pre_ref.at[j]
+        return meta_ref if j == rows else buf.at[me, j]
+
+    own_rows.wait()
 
     sent = []
 
@@ -75,9 +80,7 @@
         send(None, mine(j), me, j, across_sem.at[z, j], across)
     for j in order:
         send(None, mine(j), me, j, mate_sem.at[z * 2 + y, j], mate)
-    own_rows = pltpu.make_async_copy(pre_ref, buf.at[me], local_sem.at[1])
     own_meta = pltpu.make_async_copy(meta_ref, meta_buf.at[me], local_sem.at[2])
-    own_rows.start()
     own_meta.start()
 
     def from_across(t):
@@ -98,32 +101,31 @@
                     send(both(z == 0, has_right), slot(o, j), o, j, right_sem.at[depth, j], right)
                 send(cond, slot(o, j), o, j, mate_sem.at[zz * 2 + 1 - y, j], mate)
 
-    for s in range(1, depth):
-        for j in order:
-            for sign in (1, -1):
-                zz = z + s * sign
-                o = index(zz, y, c)
-                inside = both(zz >= 0, zz < depth)
-                pl.when(inside)(functools.partial(arrive, o, j))
-                if sign == 1:
-                    send(both(inside, has_left), slot(o, j), o, j, left_sem.at[zz, j], left)
-                else:
-                    send(both(inside, has_right), slot(o, j), o, j, right_sem.at[zz, j], right)
-                cond = both(inside, zz > 0, zz < depth - 1) if j == last else inside
-                send(cond, slot(o, j), o, j, across_sem.at[zz, j], across)
-                send(inside, slot(o, j), o, j, mate_sem.at[zz * 2 + y, j], mate)
+    def far_end(zz, here, ahead, sem, target):
+        o = index(zz, 1 - y, c)
+        pl.when(here)(functools.partial(arrive, o, last))
+        send(both(here, ahead), slot(o, last), o, last, sem.at[depth, last], target)
+        send(here, slot(o, last), o, last, mate_sem.at[zz * 2 + 1 - y, last], mate)
+
+    for s in range(1, depth + 1):
+        if s > 1:
+            far_end(depth - 1, z == depth - s, has_left, left_sem, left)
+            far_end(0, z == s - 1, has_right, right_sem, right)
+        if s < depth:
+            for j in order:
+                for sign in (1, -1):
+                    zz = z + s * sign
+                    o = index(zz, y, c)
+                    inside = both(zz >= 0, zz < depth)
+                    pl.when(inside)(functools.partial(arrive, o, j))
+                    if sign == 1:
+                        send(both(inside, has_left), slot(o, j), o, j, left_sem.at[zz, j], left)
+                    else:
+                        send(both(inside, has_right), slot(o, j), o, j, right_sem.at[zz, j], right)
+                    cond = both(inside, zz > 0, zz < depth - 1) if j == last else inside
+                    send(cond, slot(o, j), o, j, across_sem.at[zz, j], across)
+                    send(inside, slot(o, j), o, j, mate_sem.at[zz * 2 + y, j], mate)
         from_across(s - 1)
-    if depth > 1:
-        o = index(depth - 1, 1 - y, c)
-        pl.when(has_right)(functools.partial(arrive, o, last))
-        send(both(has_right, has_left), slot(o, last), o, last, left_sem.at[depth, last], left)
-        send(has_right, slot(o, last), o, last, mate_sem.at[(depth - 1) * 2 + 1 - y, last], mate)
-        o = index(0, 1 - y, c)
-        pl.when(has_left)(functools.partial(arrive, o, last))
-        send(both(has_right, has_left), slot(o, last), o, last, right_sem.at[depth, last], right)
-        send(has_left, slot(o, last), o, last, mate_sem.at[1 - y, last], mate)
-    from_across(depth - 1)
-    own_rows.wait()
     own_meta.wait()
 
     def of_mate(j):
@@ -162,14 +164,16 @@
     depth = n // 4
     dma = pltpu.SemaphoreType.DMA
     vmem = pl.BlockSpec(memory_space=pltpu.VMEM)
+    smem = pl.BlockSpec(memory_space=pltpu.SMEM)
+    hbm = pl.BlockSpec(memory_space=pltpu.HBM)
     return pl.pallas_call(
         functools.partial(gather_kernel, n),
         out_shape=(
             jax.ShapeDtypeStruct(prefill_state.shape, prefill_state.dtype),
             jax.ShapeDtypeStruct((rows,), jnp.int32),
         ),
-        in_specs=[vmem, vmem],
-        out_specs=(vmem, pl.BlockSpec(memory_space=pltpu.SMEM)),
+        in_specs=[vmem, hbm],
+        out_specs=(vmem, smem),
         scratch_shapes=[
             pltpu.VMEM((n,) + prefill_state.shape, prefill_state.dtype),
             pltpu.VMEM((n,) + meta.shape, jnp.int32),
@@ -182,38 +186,42 @@
             dma((4,)),
         ],
         compiler_params=pltpu.CompilerParams(
-            collective_id=0, has_side_effects=True, vmem_limit_bytes=ROOM + 4 * 1024 * 1024
+            collective_id=0, has_side_effects=True,
+            vmem_limit_bytes=VMEM_ALL,
+        ),
+        cost_estimate=pl.CostEstimate(
+            flops=0, bytes_accessed=16 * n * prefill_state.size * 2, transcendentals=0
         ),
         name="gather_rows",
     )(meta, prefill_state)
 
 
-def step_kernel(
-    info_ref, active_ref, cache_ref, moved_ref, weight_ref, x_ref, z_ref, b_ref, c_ref, dt_ref,
-    bias_ref, log_ref, skip_ref, gain_ref, mixed_ref, new_ref, states, fresh, weight,
-    step_rows, decay_rows, in_sem, out_sem, weight_sem,
-):
+def step_kernel(count, *refs):
+    given, (mixed_ref, new_ref), held = refs[:count], refs[count : count + 2], refs[count + 2 :]
+    (info_ref, active_ref, cache_ref, moved_ref, weight_ref, x_ref, z_ref, b_ref, c_ref, dt_ref,
+     bias_ref, log_ref, skip_ref, gain_ref) = held[:count]
+    fresh, step_rows, decay_rows, in_sem, out_sem = held[count:]
+    loads = [
+        pltpu.make_async_copy(source, target, in_sem.at[k])
+        for k, (source, target) in enumerate(zip(given, held))
+    ]
+    weights = loads[4]
+    first = loads[:2] + loads[5:]
+    for copy in first + loads[2:5]:
+        copy.start()
     slots, heads, hdim, nstate = cache_ref.shape
     inner = heads * hdim
     moves = moved_ref.shape[0]
     f32 = jnp.float32
 
-    def load(r):
+    def is_live(r):
         hit = [info_ref[j] == r for j in range(moves)]
         held = functools.reduce(jnp.logical_or, hit)
-        for j in range(moves):
-            pl.when(hit[j])(
-                pltpu.make_async_copy(moved_ref.at[j], states.at[r], in_sem.at[r]).start
-            )
-        pl.when(jnp.logical_not(held))(
-            pltpu.make_async_copy(cache_ref.at[r], states.at[r], in_sem.at[r]).start
-        )
         return jnp.where(jnp.logical_or(held, active_ref[r] > 0), 1.0, 0.0).astype(f32)
 
-    live_scalars = [load(r) for r in range(slots)]
-    weights = pltpu.make_async_copy(weight_ref, weight, weight_sem)
-    weights.start()
-
+    for copy in first:
+        copy.wait()
+    live_scalars = [is_live(r) for r in range(slots)]
     row_id = lax.broadcasted_iota(jnp.int32, (slots, 128), 0)
     live = jnp.zeros((slots, 128), f32)
     for r in range(slots):
@@ -236,11 +244,12 @@
     c = c_ref[...]
 
     def slot(r, total):
-        pltpu.make_async_copy(cache_ref.at[r], states.at[r], in_sem.at[r]).wait()
         here = row_id[:, :nstate] == r
         b_row = jnp.where(here, b.astype(f32), 0.0).astype(jnp.bfloat16)
         c_row = jnp.where(here, c.astype(f32), 0.0).astype(jnp.bfloat16)
-        state = states[r]
+        state = cache_ref[r]
+        for j in range(moves):
+            state = jnp.where(info_ref[j] == r, moved_ref[j], state)
         flat = state.reshape(inner, nstate)
         total = total + lax.dot_general(
             c_row, flat, (((1,), (1,)), ((), ())), preferred_element_type=f32
@@ -256,13 +265,15 @@
         pltpu.make_async_copy(fresh.at[r], new_ref.at[r], out_sem.at[r]).start()
         return total
 
-    held = lax.fori_loop(0, slots, slot, jnp.zeros((slots, inner), f32))
+    for copy in loads[2:4]:
+        copy.wait()
+    kept = lax.fori_loop(0, slots, slot, jnp.zeros((slots, inner), f32))
     inputs = x.astype(f32)
     mix = jnp.sum(b.astype(f32) * c.astype(f32), axis=1, keepdims=True)
-    ys = widen(decay) * held + widen(step) * inputs * mix + widen(skip_ref[...]) * inputs
+    ys = widen(decay) * kept + widen(step) * inputs * mix + widen(skip_ref[...]) * inputs
     gated = ys * jax.nn.silu(z_ref[...].astype(f32))
     scale = lax.rsqrt(jnp.mean(gated * gated, axis=1, keepdims=True) + 1e-05)
-    normed = jnp.where(live[:, :1] > 0.5, gated * scale * gain_ref[...], 0.0).astype(jnp.bfloat16)
+    normed = jnp.where(live[:, :1] > 0.5, gated * scale * gain_ref[...][None, :], 0.0).astype(jnp.bfloat16)
     weights.wait()
     width = mixed_ref.shape[1]
     tile = 512
@@ -272,7 +283,7 @@
     def columns(k, carry):
         part = pl.ds(pl.multiple_of(k * tile, tile), tile)
         mixed_ref[:, part] = jnp.dot(
-            normed, weight[:, part], preferred_element_type=f32
+            normed, weight_ref[:, part], preferred_element_type=f32
         ).astype(mixed_ref.dtype)
         return carry
 
@@ -285,39 +296,31 @@
     lax.fori_loop(0, slots, flush, 0)
 
 
-def advance(
-    info, active, cache_state, moved, out_weight, x_in, z_in, b_in, c_in, dt_in, dt_bias, a_log,
-    d_skip, norm_gain,
-):
-    slots, heads, hdim, nstate = cache_state.shape
-    vmem = pl.BlockSpec(memory_space=pltpu.VMEM)
-    smem = pl.BlockSpec(memory_space=pltpu.SMEM)
-    hbm = pl.BlockSpec(memory_space=pl.ANY)
+def advance(*given):
+    active, cache_state, out_weight, dt_in = given[1], given[2], given[4], given[9]
+    hbm = pl.BlockSpec(memory_space=pltpu.HBM)
     dma = pltpu.SemaphoreType.DMA
+    count = len(given)
     return pl.pallas_call(
-        step_kernel,
+        functools.partial(step_kernel, count),
         out_shape=(
-            jax.ShapeDtypeStruct((slots, out_weight.shape[1]), jnp.bfloat16),
+            jax.ShapeDtypeStruct((active.shape[0], out_weight.shape[1]), jnp.bfloat16),
             jax.ShapeDtypeStruct(cache_state.shape, jnp.bfloat16),
         ),
-        in_specs=[smem, smem, hbm, hbm, hbm] + [vmem] * 9,
-        out_specs=(vmem, hbm),
+        in_specs=[hbm] * count,
+        out_specs=(pl.BlockSpec(memory_space=pltpu.VMEM), hbm),
         scratch_shapes=[
-            pltpu.VMEM(cache_state.shape, cache_state.dtype),
+            *(pltpu.SMEM(a.shape, a.dtype) for a in given[:2]),
+            *(pltpu.VMEM(a.shape, a.dtype) for a in given[2:]),
             pltpu.VMEM(cache_state.shape, jnp.bfloat16),
-            pltpu.VMEM(out_weight.shape, out_weight.dtype),
-            pltpu.VMEM((slots, heads), jnp.float32),
-            pltpu.VMEM((slots, heads), jnp.float32),
-            dma((slots,)),
-            dma((slots,)),
-            dma,
+            pltpu.VMEM(dt_in.shape, jnp.float32),
+            pltpu.VMEM(dt_in.shape, jnp.float32),
+            dma((count,)),
+            dma((active.shape[0],)),
         ],
-        compiler_params=pltpu.CompilerParams(vmem_limit_bytes=32 * 1024 * 1024),
+        compiler_params=pltpu.CompilerParams(vmem_limit_bytes=VMEM_ALL),
         name="decode_step",
-    )(
-        info, active, cache_state, moved, out_weight, x_in, z_in, b_in, c_in, dt_in,
-        dt_bias[None, :], a_log[None, :], d_skip[None, :], norm_gain[None, :],
-    )
+    )(*given)
 
 
 def body(
@@ -325,12 +328,18 @@
     norm_gain, out_weight, active, prefill_count, dest_owner, dest_slot,
 ):
     rows = prefill_state.shape[0]
-    valid = jnp.arange(rows, dtype=jnp.int32) < prefill_count[0]
-    owner = jnp.where(valid, dest_owner, -1)
+    ahead = (
+        out_weight, x_in, z_in, b_in, c_in, dt_in, dt_bias[None, :],
+        a_log[None, :], d_skip[None, :], norm_gain,
+    )
     if n % 4 == 0 and n * prefill_state.size * 2 <= ROOM:
-        meta = jnp.concatenate([owner, dest_slot, jnp.zeros((128 - 2 * rows,), jnp.int32)])[None, :]
+        valid = jnp.arange(rows, dtype=jnp.int32) < prefill_count[0]
+        owner = jnp.where(valid, dest_owner, -1)
+        meta = (jnp.pad(owner, (0, 128 - rows)) + jnp.pad(dest_slot, (rows, 128 - 2 * rows)))[None, :]
         moved, info = gather_rows(meta, prefill_state, n)
     else:
+        valid = jnp.arange(rows, dtype=jnp.int32) < prefill_count[0]
+        owner = jnp.where(valid, dest_owner, -1)
         myself = lax.axis_index("batch")
         owners = lax.all_gather(owner, "batch", axis=0)
         places = lax.all_gather(dest_slot, "batch", axis=0)
@@ -340,10 +349,7 @@
         column = jnp.arange(rows)
         info = jnp.where(jnp.any(hit, axis=0), places[source, column], -1)
         moved = states[source, column]
-    return advance(
-        info, active, cache_state, moved, out_weight, x_in, z_in, b_in, c_in, dt_in, dt_bias,
-        a_log, d_skip, norm_gain,
-    )
+    return advance(info, active, cache_state, moved, *ahead)
 
 
 def solution(mesh):

time: 70.8 us -> 49.7 us (0.70)
  the two profiles are of different devices: /device:TPU:27 before, /device:TPU:1 now
where the time goes in v2:
time: 49.7 us; the launch traced here: 49.5 us
  Pallas kernels  46.3 us (93%)
  other arithmetic  1.9 us (4%)
  between operations  1.28 us (3%)
    pallas_call x1, Pallas kernels, gather_rows(): pl.pallas_call(functools.partial(gather_kernel, n), out_shape=(jax.ShapeD...  39.4 us
    pallas_call x1, Pallas kernels, advance(): pl.pallas_call(functools.partial(step_kernel, count), out_shape=(jax.Shap...  6.92 us
    broadcast_in_dim x1, other arithmetic, body(): (jnp.pad(owner, (0, 128 - rows)) + jnp.pad(dest_slot, (rows, 128 - 2 * ro...  1.24 us

profile of v2, /device:TPU:1, one launch (start us, length us, event | category | flops | bytes accessed | tf_op | source)
XLA Modules:
  0.0 49.5 jit_solution(16257073153175199917)
XLA Ops:
  1.3 0.7 %compare_select_fusion = s32[2]{0:T(128)S(1)} fusion(s32[2]{0:T(128)} %param.30, s32[]{:T(128)} %bitcast.6), kind=kLoop, calls=%fused_computation | loop fusion | flops 4 | bytes 20 | tf_op jit(solution)/shard_map/jit(_where)/select_n | solution.py:337
  1.9 1.2 %add_bitcast_fusion.meta_ref = s32[1,128]{1,0:T(1,128)} fusion(s32[2]{0:T(128)} %param.31, s32[2]{0:T(128)S(1)} %compare_select_fusion), kind=kLoop, calls=%fused_computation.1 | loop fusion | flops 128 | bytes 528 | tf_op jit(solution)/shard_map/broadcast_in_dim | solution.py:338
  3.2 39.4 %gather_rows.1 = (bf16[2,12,64,128]{3,2,1,0:T(8,128)(2,1)}, s32[2]{0:T(128)}) custom-call(s32[1,128]{1,0:T(1,128)} %add_bitcast_fusion.meta_ref, bf16[2,12,64,128]{3,2,1,0:T(8,128)(2,1)} %pre_ref.1), custom_call_target="tpu_custom_call" | custom-call | bytes 100663296 | tf_op jit(solution)/shard_map/gather_rows/pallas_call | solution.py:169
  42.5 6.9 %decode_step.1 = (bf16[8,4096]{1,0:T(8,128)(2,1)}, bf16[8,12,64,128]{3,2,1,0:T(8,128)(2,1)}) custom-call(s32[2]{0:T(128)} %get-tuple-element.4.refs_0_, s32[8]{0:T(128)} %refs_1_.1, bf16[8,12,64,128]{3,2,1,0:T(8,128)(2,1)} %refs_2_.1, bf16[2,12,64,128]{3,2,1,0:T(8,128)(2,1)} %get-tuple-element.5.refs_3_, bf16[768,4096]{1,0:T(8,128)(2,1)} %refs_4_.1, ...), custom_call_target="tpu_custom_call" | custom-call | tf_op jit(solution)/shard_map/decode_step/pallas_call | solution.py:304

commit v3 on v2

--- a/solution.py
+++ b/solution.py
@@ -13,7 +13,8 @@
 
 
 def gather_kernel(
-    n, meta_ref, pre_ref, moved_ref, info_ref, buf, meta_buf, meta_smem,
+    n, owner_ref, place_ref, count_ref, pre_ref, moved_ref, info_ref,
+    buf, owner_buf, place_buf, count_buf, owner_all, place_all, count_all,
     recv_sem, left_sem, right_sem, across_sem, mate_sem, local_sem,
 ):
     depth = n // 4
@@ -28,8 +29,14 @@
     across, mate = index(z, 1 - y, c), index(z, y, 1 - c)
     has_left, has_right = z > 0, z < depth - 1
 
-    own_rows = pltpu.make_async_copy(pre_ref, buf.at[me], local_sem.at[1])
-    own_rows.start()
+    own = [
+        pltpu.make_async_copy(source, target.at[me], local_sem.at[k])
+        for k, (source, target) in enumerate((
+            (owner_ref, owner_buf), (place_ref, place_buf), (count_ref, count_buf), (pre_ref, buf)
+        ))
+    ]
+    for copy in own:
+        copy.start()
     barrier = pltpu.get_barrier_semaphore()
 
     def greet(other):
@@ -42,12 +49,13 @@
     pl.semaphore_wait(barrier, 2 + has_left.astype(jnp.int32) + has_right.astype(jnp.int32))
 
     def slot(o, j):
-        return meta_buf.at[o] if j == rows else buf.at[o, j]
+        return buf.at[o, j] if j < rows else (owner_buf, place_buf, count_buf)[j - rows].at[o]
 
     def mine(j):
-        return meta_ref if j == rows else buf.at[me, j]
-
-    own_rows.wait()
+        return slot(me, j)
+
+    for copy in own:
+        copy.wait()
 
     sent = []
 
@@ -71,24 +79,22 @@
     def both(*conds):
         return functools.reduce(jnp.logical_and, conds)
 
-    order = (rows,) + tuple(range(rows))
+    numbers = (rows, rows + 1, rows + 2)
+    order = numbers + tuple(range(rows))
     last = rows - 1
     for j in order:
         send(has_left, mine(j), me, j, left_sem.at[z, j], left)
         send(has_right, mine(j), me, j, right_sem.at[z, j], right)
-    for j in (rows,) + tuple(reversed(range(rows))):
+    for j in numbers + tuple(reversed(range(rows))):
         send(None, mine(j), me, j, across_sem.at[z, j], across)
     for j in order:
         send(None, mine(j), me, j, mate_sem.at[z * 2 + y, j], mate)
-    own_meta = pltpu.make_async_copy(meta_ref, meta_buf.at[me], local_sem.at[2])
-    own_meta.start()
-
     def from_across(t):
         for sign in (1, -1) if t else (1,):
             zz = z + t * sign
             o = index(zz, 1 - y, c)
             inside = both(zz >= 0, zz < depth) if t else None
-            for j in (rows,) + tuple(reversed(range(rows))):
+            for j in numbers + tuple(reversed(range(rows))):
                 cond = inside
                 if t and j == last:
                     cond = both(inside, zz > 0, zz < depth - 1)
@@ -126,7 +132,6 @@
                     send(cond, slot(o, j), o, j, across_sem.at[zz, j], across)
                     send(inside, slot(o, j), o, j, mate_sem.at[zz * 2 + y, j], mate)
         from_across(s - 1)
-    own_meta.wait()
 
     def of_mate(j):
         def one(k, carry):
@@ -134,17 +139,25 @@
             return carry
         lax.fori_loop(0, 2 * depth, one, 0)
 
-    of_mate(rows)
-    numbers = pltpu.make_async_copy(meta_buf, meta_smem, local_sem.at[3])
-    numbers.start()
-    numbers.wait()
+    for j in numbers:
+        of_mate(j)
+    reads = [
+        pltpu.make_async_copy(source, target, local_sem.at[k])
+        for k, (source, target) in enumerate((
+            (owner_buf, owner_all), (place_buf, place_all), (count_buf, count_all)
+        ))
+    ]
+    for copy in reads:
+        copy.start()
+    for copy in reads:
+        copy.wait()
 
     picks = []
     for j in range(rows):
         def look(d, carry, j=j):
-            hit = meta_smem[d, 0, j] == me
+            hit = jnp.logical_and(owner_all[d, 0, j] == me, count_all[d, 0, 0] > j)
             source, place = carry
-            return jnp.where(hit, d, source), jnp.where(hit, meta_smem[d, 0, rows + j], place)
+            return jnp.where(hit, d, source), jnp.where(hit, place_all[d, 0, j], place)
         source, place = lax.fori_loop(0, n, look, (jnp.int32(0), jnp.int32(-1)))
         picks.append(source)
         info_ref[j] = place
@@ -159,7 +172,7 @@
             pl.when(cond)(copy.wait_send)
 
 
-def gather_rows(meta, prefill_state, n):
+def gather_rows(owner, place, live_rows, prefill_state, n):
     rows = prefill_state.shape[0]
     depth = n // 4
     dma = pltpu.SemaphoreType.DMA
@@ -172,17 +185,17 @@
             jax.ShapeDtypeStruct(prefill_state.shape, prefill_state.dtype),
             jax.ShapeDtypeStruct((rows,), jnp.int32),
         ),
-        in_specs=[vmem, hbm],
+        in_specs=[hbm] * 4,
         out_specs=(vmem, smem),
         scratch_shapes=[
             pltpu.VMEM((n,) + prefill_state.shape, prefill_state.dtype),
-            pltpu.VMEM((n,) + meta.shape, jnp.int32),
-            pltpu.SMEM((n,) + meta.shape, jnp.int32),
-            dma((n, rows + 1)),
-            dma((depth + 1, rows + 1)),
-            dma((depth + 1, rows + 1)),
-            dma((depth, rows + 1)),
-            dma((2 * depth, rows + 1)),
+            *(pltpu.VMEM((n,) + a.shape, jnp.int32) for a in (owner, place, live_rows)),
+            *(pltpu.SMEM((n,) + a.shape, jnp.int32) for a in (owner, place, live_rows)),
+            dma((n, rows + 3)),
+            dma((depth + 1, rows + 3)),
+            dma((depth + 1, rows + 3)),
+            dma((depth, rows + 3)),
+            dma((2 * depth, rows + 3)),
             dma((4,)),
         ],
         compiler_params=pltpu.CompilerParams(
@@ -193,7 +206,7 @@
             flops=0, bytes_accessed=16 * n * prefill_state.size * 2, transcendentals=0
         ),
         name="gather_rows",
-    )(meta, prefill_state)
+    )(owner, place, live_rows, prefill_state)
 
 
 def step_kernel(count, *refs):
@@ -333,10 +346,9 @@
         a_log[None, :], d_skip[None, :], norm_gain,
     )
     if n % 4 == 0 and n * prefill_state.size * 2 <= ROOM:
-        valid = jnp.arange(rows, dtype=jnp.int32) < prefill_count[0]
-        owner = jnp.where(valid, dest_owner, -1)
-        meta = (jnp.pad(owner, (0, 128 - rows)) + jnp.pad(dest_slot, (rows, 128 - 2 * rows)))[None, :]
-        moved, info = gather_rows(meta, prefill_state, n)
+        moved, info = gather_rows(
+            dest_owner[None, :], dest_slot[None, :], prefill_count[None, :], prefill_state, n
+        )
     else:
         valid = jnp.arange(rows, dtype=jnp.int32) < prefill_count[0]
         owner = jnp.where(valid, dest_owner, -1)

time: 49.7 us -> 48.3 us (0.972)
  other arithmetic: 1.9 us -> 0 us
  Pallas kernels: 46.3 us -> 46.9 us
    broadcast_in_dim x1 -> x0, other arithmetic: 1.24 us -> none  [body(): (jnp.pad(owner, (0, 128 - rows)) + jnp.pad(dest_slot, (rows, 128 - 2 * ro...]
    select_n x1 -> x0, other arithmetic: 0.66 us -> none  [body(): owner = jnp.where(valid, dest_owner, -1)]
    pallas_call x1, Pallas kernels: 39.4 us -> 39.9 us  [gather_rows(): pl.pallas_call(functools.partial(gather_kernel, n), out_shape=(jax.ShapeD...]
where the time goes in v3:
time: 48.3 us; the launch traced here: 48.2 us
  Pallas kernels  46.9 us (97%)
  between operations  1.28 us (3%)
    pallas_call x1, Pallas kernels, gather_rows(): pl.pallas_call(functools.partial(gather_kernel, n), out_shape=(jax.ShapeD...  39.9 us
    pallas_call x1, Pallas kernels, advance(): pl.pallas_call(functools.partial(step_kernel, count), out_shape=(jax.Shap...  6.92 us

profile of v3, /device:TPU:1, one launch (start us, length us, event | category | flops | bytes accessed | tf_op | source)
XLA Modules:
  0.0 48.2 jit_solution(3339122954787801974)
XLA Ops:
  1.3 39.9 %gather_rows.1 = (bf16[2,12,64,128]{3,2,1,0:T(8,128)(2,1)}, s32[2]{0:T(128)}) custom-call(s32[1,2]{1,0:T(1,128)} %bitcast.7, s32[1,2]{1,0:T(1,128)} %bitcast.8, s32[1,1]{1,0:T(1,128)} %bitcast.6.count_ref, bf16[2,12,64,128]{3,2,1,0:T(8,128)(2,1)} %pre_ref.1), custom_call_target="tpu_custom_call" | custom-call | bytes 100663296 | tf_op jit(solution)/shard_map/gather_rows/pallas_call | solution.py:182
  41.2 6.9 %decode_step.1 = (bf16[8,4096]{1,0:T(8,128)(2,1)}, bf16[8,12,64,128]{3,2,1,0:T(8,128)(2,1)}) custom-call(s32[2]{0:T(128)} %get-tuple-element.4.refs_0_, s32[8]{0:T(128)} %refs_1_.1, bf16[8,12,64,128]{3,2,1,0:T(8,128)(2,1)} %refs_2_.1, bf16[2,12,64,128]{3,2,1,0:T(8,128)(2,1)} %get-tuple-element.5.refs_3_, bf16[768,4096]{1,0:T(8,128)(2,1)} %refs_4_.1, ...), custom_call_target="tpu_custom_call" | custom-call | tf_op jit(solution)/shard_map/decode_step/pallas_call | solution.py:317
